TPU v7x, 256 devices: a whole 4x4x8 slice. The times are simulated.
256 devices in a mesh: seq: 64 (over x, z, core), head: 4 (over y).
Axes of the slice: x: 4, y: 4, z: 8, core: 2. Of those that a mesh axis runs over, the one named last changes fastest.
Arguments:
- queries: bfloat16 [16384, 64, 128], P('seq', 'head'), may hold values from -360 to 360
- head_weights: bfloat16 [16384, 64], P('seq', 'head'), may hold values from -0.75 to 0.75
- keys: bfloat16 [16384, 128], P('seq'), may hold values from -6 to 6
- targets: bfloat16 [16384, 2048], P('seq'), may hold values from 0.0099487305 to 10
- chosen: int32 [128, 16], P('seq'), may hold values from -1 to 127, as said below
- tile_block: int32 [128], replicated, may hold values from 0 to 127, as said below
Outputs:
- query_grads: bfloat16 [16384, 64, 128], P('seq', 'head')
- weight_grads: float32 [16384, 64], P('seq', 'head')
- key_grads: float32 [16384, 128], P('seq')
- loss: float32 [], replicated
Inputs may be any that keep to these rules, and one draw needn't show every extreme that they name: `tile_block`: a permutation of 0 to 127; each aligned group of 4 stored positions holds the global blocks of that same group. `chosen`: slot 0 of stored tile p is tile_block[p]; live entries of a row are distinct, none exceeds tile_block[p], and they precede the -1 entries; over all tiles of one device of seq, at most 1 distinct live block is stored on any one other device.
All inputs are finite; a program needn't handle non-finite values.
Results may differ from a plain program's by a relative error of at most 0.0095.
Values may be sent and summed in bfloat16 or wider, within the bound.
A program may use at most 128 MiB of HBM per device.

v0:
```python
import jax
import jax.numpy as jnp
from jax import lax
from jax.sharding import Mesh
from jax.sharding import PartitionSpec as P

BLOCK = 128
SLOTS = 16
CAP = 1
KEYS = 2048
SEQ = ("seq_0", "seq_1", "seq_2")
SEQ_HEAD = ("seq_0", "seq_1", "seq_2", "head")
loss_scale = 4194304.0


def over_axes(value, axes):
    for axis in axes:
        value = lax.psum(value, axis)
    return value


def copy_for_each(value, axis):
    copies = jnp.broadcast_to(value, (lax.axis_size(axis), *value.shape))
    return lax.all_to_all(copies, axis, split_axis=0, concat_axis=0, tiled=True)


def over_copies(value, axis):
    return copy_for_each(value, axis).astype(jnp.float32).sum(axis=0)


def row_statistics(score_part, mask_part, target_part):
    row_max = jnp.max(jnp.where(mask_part, score_part, -1e30), axis=1)
    exp_terms = jnp.where(
        mask_part, jnp.exp(jnp.where(mask_part, score_part - row_max[:, None], 0.0)), 0.0
    )
    return (row_max, jnp.sum(exp_terms, axis=1), jnp.sum(target_part, axis=1))


def local(queries, head_weights, keys, targets, chosen, tile_block):
    row_count, heads_here, key_width = queries.shape
    tiles_here = row_count // BLOCK
    block_count = tile_block.shape[0]
    owner_count = block_count // tiles_here
    score_scale = key_width ** (-0.5)
    seq_index = lax.axis_index(SEQ)
    head_index = lax.axis_index("head")
    is_first = (head_index == 0).astype(jnp.float32)
    positions = jnp.arange(block_count, dtype=jnp.int32)
    home_of = jnp.sum(
        jnp.where(tile_block[None, :] == positions[:, None], positions[None, :], 0), axis=1
    )
    live_slot = chosen >= 0
    position = home_of[jnp.maximum(chosen, 0)]
    owner_index = position // tiles_here
    local_slot = position % tiles_here
    own_block = lax.dynamic_slice_in_dim(tile_block, seq_index * tiles_here, tiles_here)
    offsets = jnp.arange(BLOCK, dtype=jnp.int32)
    causal = offsets[None, :] <= offsets[:, None]
    own_slot = chosen == own_block[:, None]
    live_mask = live_slot[:, None, :, None] & (
        (~own_slot)[:, None, :, None] | causal[None, :, None, :]
    )
    live_mask = live_mask.reshape(row_count, KEYS)
    key_blocks = keys.reshape(tiles_here, BLOCK, key_width)
    remote = live_slot & (owner_index != seq_index)
    remote_pos = jnp.where(remote, position, -1).reshape(-1)
    wanted = jnp.any(remote_pos[:, None] == positions[None, :], axis=0).reshape(
        owner_count, tiles_here
    )
    slot_rank = jnp.cumsum(wanted.astype(jnp.int32), axis=1) - 1
    local_iota = jnp.arange(tiles_here, dtype=jnp.int32)
    request = jnp.stack(
        [jnp.sum(jnp.where(wanted & (slot_rank == 0), local_iota[None, :], 0), axis=1)], axis=1
    )
    asked_slots = lax.all_to_all(request, SEQ, split_axis=0, concat_axis=0, tiled=True)
    reply_blocks = key_blocks[asked_slots]
    arrived = lax.all_to_all(reply_blocks, SEQ, split_axis=0, concat_axis=0, tiled=True)
    key_table = jnp.concatenate(
        [key_blocks, arrived.reshape(owner_count * CAP, BLOCK, key_width)], axis=0
    )
    table_index = jnp.where(
        owner_index == seq_index,
        local_slot,
        tiles_here + owner_index * CAP + slot_rank[owner_index, local_slot],
    )
    table_index = jnp.where(live_slot, table_index, 0)
    fetched = key_table[table_index]
    query_tiles = queries.reshape(tiles_here, BLOCK, heads_here, key_width)
    weight_tiles = head_weights.astype(jnp.float32).reshape(tiles_here, BLOCK, heads_here)

    def dot_values(query_tile, key_tile):
        return jnp.einsum(
            "qhd,kd->qhk",
            query_tile,
            key_tile.reshape(-1, key_width),
            preferred_element_type=jnp.float32,
        )

    def forward(operands):
        query_tile, weight_tile, key_tile = operands
        values = dot_values(query_tile, key_tile)
        return score_scale * jnp.sum(jnp.maximum(values, 0.0) * weight_tile[:, :, None], axis=1)

    partial_value = lax.map(forward, (query_tiles, weight_tiles, fetched)).reshape(row_count, KEYS)
    target_vals = jnp.where(live_mask, targets.astype(jnp.float32), 0.0)
    pair_local = jnp.sum(live_mask.astype(jnp.float32))
    score_part = lax.psum(partial_value, "head")
    row_max, row_norm, row_target = row_statistics(score_part, live_mask, target_vals)
    target_prob = jnp.where(live_mask, target_vals / row_target[:, None], 0.0)
    kl_cols = jnp.sum(
        jnp.where(
            live_mask,
            target_prob * (jnp.log(jnp.where(live_mask, target_prob, 1.0)) - score_part),
            0.0,
        )
    )
    lse_sum = jnp.sum(row_max + jnp.log(row_norm))
    loss_part = is_first * (kl_cols + lse_sum)
    loss_total, pair_count = (
        over_axes(loss_part, SEQ_HEAD),
        over_axes(is_first * pair_local, SEQ_HEAD),
    )
    softmax_vals = (
        jnp.where(live_mask, jnp.exp(jnp.where(live_mask, score_part - row_max[:, None], 0.0)), 0.0)
        / row_norm[:, None]
    )
    grad_part = loss_scale * KEYS * (softmax_vals - target_prob) / pair_count
    grad_tiles = grad_part.reshape(tiles_here, BLOCK, KEYS)

    def backward(operands):
        query_tile, weight_tile, key_tile, grad_tile = operands
        key_rows = key_tile.reshape(-1, key_width)
        values = dot_values(query_tile, key_tile)
        weight_grad = score_scale * jnp.sum(
            jnp.maximum(values, 0.0) * grad_tile[:, None, :], axis=2
        )
        dot_grads = (
            score_scale
            * weight_tile[:, :, None]
            * grad_tile[:, None, :]
            * (values > 0).astype(jnp.float32)
        ).astype(jnp.bfloat16)
        query_grad = jnp.einsum(
            "qhk,kd->qhd", dot_grads, key_rows, preferred_element_type=jnp.float32
        ).astype(jnp.bfloat16)
        key_grad = jnp.einsum(
            "qhk,qhd->kd", dot_grads, query_tile, preferred_element_type=jnp.float32
        )
        return (query_grad, weight_grad, key_grad.reshape(SLOTS, BLOCK, key_width))

    query_grads, weight_grads, key_parts = lax.map(
        backward, (query_tiles, weight_tiles, fetched, grad_tiles)
    )
    slot_grads = key_parts.reshape(tiles_here * SLOTS, BLOCK, key_width)
    spread = jax.ops.segment_sum(
        slot_grads, table_index.reshape(-1), num_segments=tiles_here + owner_count * CAP
    )
    returned = lax.all_to_all(
        spread[tiles_here:].reshape(owner_count, CAP, BLOCK, key_width).astype(jnp.bfloat16),
        SEQ,
        split_axis=0,
        concat_axis=0,
        tiled=True,
    ).astype(jnp.float32)
    owned_grad = spread[:tiles_here] + jax.ops.segment_sum(
        returned.reshape(owner_count * CAP, BLOCK, key_width),
        asked_slots.reshape(-1),
        num_segments=tiles_here,
    )
    key_grads = over_copies(owned_grad.astype(jnp.bfloat16), "head").astype(jnp.float32)
    return (
        query_grads.reshape(row_count, heads_here, key_width),
        weight_grads.reshape(row_count, heads_here),
        key_grads.reshape(row_count, key_width),
        KEYS * loss_total / pair_count,
    )


def solution(mesh):
    torus = Mesh(
        mesh.devices.reshape(4, 8, 2, mesh.shape["head"]), ("seq_0", "seq_1", "seq_2", "head")
    )
    in_specs = (P(SEQ, "head", None), P(SEQ, "head"), P(SEQ, None), P(SEQ, None), P(SEQ, None), P())
    out_specs = (P(SEQ, "head", None), P(SEQ, "head"), P(SEQ, None), P())
    return jax.shard_map(local, mesh=torus, in_specs=in_specs, out_specs=out_specs, check_vma=False)
```

profile of v0, /device:TPU:1, one launch (start us, length us, event | category | flops | bytes accessed | tf_op | source)
XLA Modules:
  0.0 379.5 jit_solution(12548023386545640363)
XLA Ops:
  7.2 0.8 select_reduce_fusion.2
  11.0 22.1 %all_to_all.27 = s32[64,1,1]{2,1,0:T(1,128)S(1)} all-to-all(s32[64,1,1]{2,1,0:T(1,128)S(1)} %copy.39), channel_id=1, replica_groups=mesh['seq_0'=4,'seq_1'=8,'seq_2'=2,'head'=4] {'seq_0','seq_1','seq_2'}, dimensions={0} | all-to-all | bytes 512 | tf_op jit(solution)/shard_map/all_to_all | solution.py:75
  33.1 2.7 fusion.46
  35.8 2.2 gather_fusion.1
  37.9 5.7 %all-to-all-start.1 = ((bf16[64,1,128,128]{3,2,1,0:T(8,128)(2,1)}), bf16[64,1,128,128]{3,2,1,0:T(8,128)(2,1)}, u32[]{:S(2)}, u32[]{:S(2)}) async-start(bf16[64,1,128,128]{3,2,1,0:T(8,128)(2,1)} %bitcast.22), calls=%async_computation.1 | async-start | bytes 4194304 | tf_op jit(solution)/shard_map/all_to_all | solution.py:77
  43.9 0.7 gather_fusion.2
  45.1 49.8 %all-to-all-done.1 = bf16[64,1,128,128]{3,2,1,0:T(8,128)(2,1)} async-done(((bf16[64,1,128,128]{3,2,1,0:T(8,128)(2,1)}), bf16[64,1,128,128]{3,2,1,0:T(8,128)(2,1)}, u32[]{:S(2)}, u32[]{:S(2)}) %all-to-all-start.1) | async-done | bytes 2097184 | tf_op jit(solution)/shard_map/all_to_all | solution.py:77
  94.9 3.1 pad_maximum_fusion
  98.0 2.4 gather_fusion.3
  100.4 8.3 %while.24 = (s32[]{:T(128)}, f32[2,128,2048]{2,1,0:T(8,128)}, bf16[2,128,16,128]{3,1,2,0:T(8,128)(2,1)S(1)}, bf16[2,16,128,128]{3,2,1,0:T(8,128)(2,1)S(1)}, f32[2,128,16]{1,2,0:T(8,128)S(1)}, /*index=5*/s32[]{:T(128)}) while((s32[]{:T(128)}, f32[2,128,2048]{2,1,0:T(8,128)}, bf16[2,128,16,128]{3,1,2,0:T(8,128)(2,1)S(1)}, ...), condition=%wide.region_6.7_spmd, body=%wide.region_4.6_spmd.sunk | while | flops 1086324736 | bytes 22044820 | solution.py:104
  100.5 2.6 multiply_reduce_fusion.4
  103.3 1.3 copy-done.8
  104.6 2.6 multiply_reduce_fusion.4
  107.4 1.3 copy-done.8
  109.5 1.3 convert_reduce_fusion
  111.5 1.2 or_and_fusion
  112.7 56.5 %all-reduce.6.cloned.1.call-done = f32[256,2048]{1,0:T(8,128)} async-done(((f32[256,2048]{1,0:T(8,128)}), f32[256,2048]{1,0:T(8,128)}) %all-reduce.6.cloned.1.call-update) | async-done | bytes 2097168 | tf_op jit(solution)/shard_map/psum | solution.py:107
  169.2 2.9 select_reduce_fusion.1
  172.1 3.6 select_reduce_fusion
  178.4 8.9 %all-reduce.2 = (f32[]{:T(128)}, f32[]{:T(128)}) all-reduce(f32[]{:T(128)S(6)} %mul.113, f32[]{:T(128)S(6)} %mul.115), channel_id=1, replica_groups=mesh['seq_0'=4,'seq_1'=8,'seq_2'=2,'head'=4] {'seq_0'}, use_global_device_ids=true, to_apply=%region_12.13 | all-reduce | flops 2 | bytes 16 | tf_op jit(solution)/shard_map/psum | solution.py:18
  187.3 14.4 %all-reduce = (f32[]{:T(128)}, f32[]{:T(128)}) all-reduce(f32[]{:T(128)} %get-tuple-element.167, f32[]{:T(128)} %get-tuple-element.168), channel_id=1, replica_groups=mesh['seq_0'=4,'seq_1'=8,'seq_2'=2,'head'=4] {'seq_1'}, use_global_device_ids=true, to_apply=%region_13.14 | all-reduce | flops 2 | bytes 16 | tf_op jit(solution)/shard_map/psum | solution.py:18
  201.7 9.4 %all-reduce.3 = (f32[]{:T(128)}, f32[]{:T(128)}) all-reduce(f32[]{:T(128)} %get-tuple-element.163, f32[]{:T(128)} %get-tuple-element.164), channel_id=1, replica_groups=mesh['seq_0'=4,'seq_1'=8,'seq_2'=2,'head'=4] {'seq_2'}, use_global_device_ids=true, to_apply=%region_14.15 | all-reduce | flops 2 | bytes 16 | tf_op jit(solution)/shard_map/psum | solution.py:18
  211.1 7.4 %all-reduce.1 = (f32[]{:T(128)}, f32[]{:T(128)}) all-reduce(f32[]{:T(128)} %get-tuple-element.169, f32[]{:T(128)} %get-tuple-element.170), channel_id=1, replica_groups=mesh['seq_0'=4,'seq_1'=8,'seq_2'=2,'head'=4] {'head'}, use_global_device_ids=true, to_apply=%region_15.16 | all-reduce | flops 2 | bytes 16 | tf_op jit(solution)/shard_map/psum | solution.py:18
  218.4 4.8 %multiply_divide_fusion = f32[256,2048]{1,0:T(8,128)} fusion(f32[256,2048]{1,0:T(8,128)S(1)} %copy-done.1, bf16[256,2048]{1,0:T(8,128)(2,1)} %param.13, f32[]{:T(128)} %get-tuple-element.165, f32[256]{0:T(256)S(1)} %get-tuple-element.134, f32[256]{0:T(256)S(1)} %get-tuple-element.132, f32[256]{0:T(256)S(1)} %get-tuple-element.133, ...), kind=kLoop, calls=%fused_computation.54 | loop fusion | flops 5767168 | bytes 5770244 | tf_op jit(solution)/shard_map/div | solution.py:127
  223.2 54.7 %while.25 = (s32[]{:T(128)}, bf16[2,128,16,128]{3,2,1,0:T(8,128)(2,1)}, f32[2,128,16]{1,0,2:T(2,128)S(1)}, f32[2,16,128,128]{3,2,1,0:T(8,128)}, bf16[2,128,16,12...) while((s32[]{:T(128)}, ...), condition=%wide.region_18.19_spmd, body=%wide.region_16.18_spmd.sunk | while | flops 3313502208 | bytes 53560508 | solution.py:151
  223.3 1.6 dynamic-slice_bitcast_fusion.6
  224.9 7.1 %fusion.74 = (u16[128,2048]{1,0:T(8,128)(2,1)S(1)}, f32[128,16,2048]{2,0,1:T(8,128)}) fusion(bf16[2048,128,1]{1,0,2:T(8,128)(2,1)S(1)} %bitcast.149, bf16[2,128,16,128]{3,1,2,0:T(8,128)(2,1)S(1)} %copy-done.4, s32[]{:T(128)S(6)} %copy.100), kind=kOutput, calls=%fused_computation.21.clone.1 | convolution fusion | flops 1094451200 | bytes 18350084 | tf_op jit(solution)/shard_map/while/body/eval_jaxpr/qhd,kd->qhk/dot_general | solution.py:92
  232.0 3.4 fusion.75
  235.4 7.5 %multiply_reduce_fusion.5 = f32[128,16]{0,1:T(8,128)S(1)} fusion(f32[128,16,2048]{2,0,1:T(8,128)} %get-tuple-element.272, f32[128,2048]{1,0:T(8,128)S(1)} %get-tuple-element.269), kind=kLoop, calls=%fused_computation.19.clone.1 | loop fusion | flops 12580864 | bytes 17833984 | tf_op jit(solution)/shard_map/while/body/eval_jaxpr/reduce_sum | solution.py:134
  243.0 2.2 copy_dynamic-update-slice_fusion.2
  245.1 5.4 %fusion.76 = f32[2,16,128,128]{3,2,1,0:T(8,128)} fusion(f32[2,16,128,128]{3,2,1,0:T(8,128)} %get-tuple-element.306, s32[]{:T(128)S(6)} %copy.100, bf16[2,128,16,128]{3,1,2,0:T(8,128)(2,1)} %get-tuple-element.317, f32[2048,128]{0,1:T(8,128)S(1)} %get-tuple-element.273, f32[16,128]{1,0:T(8,128)S(1)} %get-tuple-element.274, u16[128,2048]{1,0:T(8,128)(2,1)} %copy-done.2), kind=kOutput, calls=%fused_computation.28.clone.1 | convolution fusion | flops 1103101952 | bytes 3154944 | tf_op jit(solution)/shard_map/while/body/eval_jaxpr/qhk,qhd->kd/dot_general | solution.py:146
  250.6 1.6 dynamic-slice_bitcast_fusion.6
  252.2 7.1 %fusion.74 = (u16[128,2048]{1,0:T(8,128)(2,1)S(1)}, f32[128,16,2048]{2,0,1:T(8,128)}) fusion(bf16[2048,128,1]{1,0,2:T(8,128)(2,1)S(1)} %bitcast.149, bf16[2,128,16,128]{3,1,2,0:T(8,128)(2,1)S(1)} %copy-done.4, s32[]{:T(128)S(6)} %copy.100), kind=kOutput, calls=%fused_computation.21.clone.1 | convolution fusion | flops 1094451200 | bytes 18350084 | tf_op jit(solution)/shard_map/while/body/eval_jaxpr/qhd,kd->qhk/dot_general | solution.py:92
  259.4 3.4 fusion.75
  262.8 7.5 %multiply_reduce_fusion.5 = f32[128,16]{0,1:T(8,128)S(1)} fusion(f32[128,16,2048]{2,0,1:T(8,128)} %get-tuple-element.272, f32[128,2048]{1,0:T(8,128)S(1)} %get-tuple-element.269), kind=kLoop, calls=%fused_computation.19.clone.1 | loop fusion | flops 12580864 | bytes 17833984 | tf_op jit(solution)/shard_map/while/body/eval_jaxpr/reduce_sum | solution.py:134
  270.3 2.2 copy_dynamic-update-slice_fusion.2
  272.5 5.4 %fusion.76 = f32[2,16,128,128]{3,2,1,0:T(8,128)} fusion(f32[2,16,128,128]{3,2,1,0:T(8,128)} %get-tuple-element.306, s32[]{:T(128)S(6)} %copy.100, bf16[2,128,16,128]{3,1,2,0:T(8,128)(2,1)} %get-tuple-element.317, f32[2048,128]{0,1:T(8,128)S(1)} %get-tuple-element.273, f32[16,128]{1,0:T(8,128)S(1)} %get-tuple-element.274, u16[128,2048]{1,0:T(8,128)(2,1)} %copy-done.2), kind=kOutput, calls=%fused_computation.28.clone.1 | convolution fusion | flops 1103101952 | bytes 3154944 | tf_op jit(solution)/shard_map/while/body/eval_jaxpr/qhk,qhd->kd/dot_general | solution.py:146
  277.9 2.5 broadcast_in_dim.112
  280.5 6.9 %scatter_fusion = f32[66,128,128]{2,1,0:T(8,128)} fusion(f32[66,128,128]{2,1,0:T(8,128)} %broadcast_in_dim.112, s32[32]{0:T(128)S(1)} %copy-done.13, f32[32,128,128]{2,1,0:T(8,128)S(1)} %bitcast.157), kind=kCustom, calls=%fused_computation.4 | custom fusion | flops 524288 | bytes 6291584 | tf_op jit(solution)/shard_map/scatter-add | solution.py:155
  287.4 3.9 %fusion.37 = bf16[64,1,128,128]{3,2,1,0:T(8,128)(2,1)} fusion(f32[66,128,128]{2,1,0:T(8,128)} %scatter_fusion), kind=kLoop, calls=%fused_computation.50 | loop fusion | bytes 4194304 | tf_op jit(solution)/shard_map/convert_element_type | solution.py:159
  291.3 6.9 %all-to-all-start.2 = ((bf16[64,1,128,128]{3,2,1,0:T(8,128)(2,1)}), bf16[64,1,128,128]{3,2,1,0:T(8,128)(2,1)S(1)}, u32[]{:S(2)}, u32[]{:S(2)}) async-start(bf16[64,1,128,128]{3,2,1,0:T(8,128)(2,1)} %fusion.37), calls=%async_computation.2 | async-start | bytes 4194304 | tf_op jit(solution)/shard_map/all_to_all | solution.py:158
  298.2 0.9 slice.17
  299.2 50.3 %all-to-all-done.2 = bf16[64,1,128,128]{3,2,1,0:T(8,128)(2,1)S(1)} async-done(((bf16[64,1,128,128]{3,2,1,0:T(8,128)(2,1)}), bf16[64,1,128,128]{3,2,1,0:T(8,128)(2,1)S(1)}, u32[]{:S(2)}, u32[]{:S(2)}) %all-to-all-start.2) | async-done | bytes 2097184 | tf_op jit(solution)/shard_map/all_to_all | solution.py:158
  349.4 2.5 bitcast_convert_fusion
  351.9 8.8 %scatter_fusion.1 = f32[2,128,128]{2,1,0:T(8,128)S(1)} fusion(f32[2,128,128]{2,1,0:T(8,128)S(1)} %slice.17, s32[64]{0:T(128)S(1)} %copy-done.12, f32[64,128,128]{2,1,0:T(8,128)} %bitcast_convert_fusion), kind=kCustom, calls=%fused_computation.5 | custom fusion | flops 1048576 | bytes 12583168 | tf_op jit(solution)/shard_map/scatter-add | solution.py:165
  360.7 0.7 broadcast_in_dim.113
  361.4 3.4 all-to-all-start.3
  366.8 4.1 %all-to-all-done.3 = bf16[4,2,128,128]{3,2,1,0:T(8,128)(2,1)S(1)} async-done(((bf16[4,2,128,128]{3,2,1,0:T(8,128)(2,1)}), bf16[4,2,128,128]{3,2,1,0:T(8,128)(2,1)S(1)}, u32[]{:S(2)}, u32[]{:S(2)}) %all-to-all-start.3) | async-done | bytes 262176 | tf_op jit(solution)/shard_map/all_to_all | solution.py:24
  (87 shorter events, 7.6 us)
Async XLA Ops:
  7.2 28.6 %copy-start = (bf16[256,128]{1,0:T(8,128)(2,1)S(1)}, bf16[256,128]{1,0:T(8,128)(2,1)}, u32[]{:S(2)}) copy-start(bf16[256,128]{1,0:T(8,128)(2,1)} %param.12) | copy-start | bytes 196612
  37.9 6.9 %copy-start.9 = (bf16[256,16,128]{2,1,0:T(8,128)(2,1)S(1)}, bf16[256,16,128]{2,1,0:T(8,128)(2,1)}, u32[]{:S(2)}) copy-start(bf16[256,16,128]{2,1,0:T(8,128)(2,1)} %param.10) | copy-start | bytes 3145732
  37.9 57.0 %all-to-all-start.1 = ((bf16[64,1,128,128]{3,2,1,0:T(8,128)(2,1)}), bf16[64,1,128,128]{3,2,1,0:T(8,128)(2,1)}, u32[]{:S(2)}, u32[]{:S(2)}) async-start(bf16[64,1,128,128]{3,2,1,0:T(8,128)(2,1)} %bitcast.22), calls=%async_computation.1 | async-start | bytes 4194304 | tf_op jit(solution)/shard_map/all_to_all | solution.py:77
  43.7 1.4 copy-start.11
  43.7 125.5 %all-reduce.6.cloned.1.call-start = ((), (), s32[]{:S(2)}) async-start(), calls=%async_computation.4 | async-start | bytes 4194304 | tf_op jit(solution)/shard_map/psum | solution.py:107
  100.5 2.7 copy-start.7
  103.3 1.3 copy-start.8
  104.6 2.7 copy-start.7
  107.4 1.3 copy-start.8
  108.7 3.9 %copy-start.3 = (bf16[2,128,16,128]{3,1,2,0:T(8,128)(2,1)}, bf16[2,128,16,128]{3,1,2,0:T(8,128)(2,1)S(1)}, u32[]{:S(2)}) copy-start(bf16[2,128,16,128]{3,1,2,0:T(8,128)(2,1)S(1)} %get-tuple-element.326) | copy-start | bytes 3145732
  108.7 0.7 copy-start.14
  108.7 0.7 copy-start.10
  169.2 2.9 copy-start.1
  169.2 2.9 copy-start.5
  223.2 1.6 copy-start.4
  232.0 3.4 copy-start.2
  250.6 1.6 copy-start.4
  259.4 3.4 copy-start.2
  277.9 2.5 copy-start.6
  277.9 2.5 copy-start.13
  291.3 58.1 %all-to-all-start.2 = ((bf16[64,1,128,128]{3,2,1,0:T(8,128)(2,1)}), bf16[64,1,128,128]{3,2,1,0:T(8,128)(2,1)S(1)}, u32[]{:S(2)}, u32[]{:S(2)}) async-start(bf16[64,1,128,128]{3,2,1,0:T(8,128)(2,1)} %fusion.37), calls=%async_computation.2 | async-start | bytes 4194304 | tf_op jit(solution)/shard_map/all_to_all | solution.py:158
  299.1 52.7 %copy-start.12 = (s32[64]{0:T(128)S(1)}, s32[64]{0:T(128)}, u32[]{:S(2)}) copy-start(s32[64]{0:T(128)} %get-tuple-element.135) | copy-start | bytes 772
  361.4 9.4 %all-to-all-start.3 = ((bf16[4,2,128,128]{3,2,1,0:T(8,128)(2,1)}), bf16[4,2,128,128]{3,2,1,0:T(8,128)(2,1)S(1)}, u32[]{:S(2)}, u32[]{:S(2)}) async-start(bf16[4,2,128,128]{3,2,1,0:T(8,128)(2,1)} %broadcast_in_dim.113), calls=%async_computation.3 | async-start | bytes 524288 | tf_op jit(solution)/shard_map/all_to_all | solution.py:24
Sparse Core Ops, SparseCore 0:
  108.9 60.2 all-reduce.5
where the time goes:
time: 381 us; the launch traced here: 380 us
  waiting for transfers between devices  161 us (42%)
  blocking collectives  62.1 us (16%)
  other arithmetic  57.1 us (15%)
  matrix products  37.2 us (10%)
  local copies, waits for them, and re-layouts  27.4 us (7%)
  between operations  18.7 us (5%)
  starting transfers between devices  16.1 us (4%)
    psum x1, waiting for transfers between devices, local(): score_part = lax.psum(partial_value, 'head')  56.5 us
    all_to_all x1, waiting for transfers between devices, local(): lax.all_to_all(spread[tiles_here:].reshape(owner_count, CAP, BLOCK, key_w...  50.3 us
    all_to_all x1, waiting for transfers between devices, local(): lax.all_to_all(reply_blocks, SEQ, split_axis=0, concat_axis=0, tiled=True)  49.8 us
    psum x4, blocking collectives, over_axes(): value = lax.psum(value, axis)  40 us
    all_to_all x1, blocking collectives, local(): lax.all_to_all(request, SEQ, split_axis=0, concat_axis=0, tiled=True)  22.1 us
    dot_general x4, matrix products, dot_values(): jnp.einsum('qhd,kd->qhk', query_tile, key_tile.reshape(-1, key_width), pr...  19.5 us
    reduce_sum x2, other arithmetic, backward(): jnp.sum(jnp.maximum(values, 0.0) * grad_tile[:, None, :], axis=2)  14.9 us
    dot_general x2, matrix products, backward(): jnp.einsum('qhk,qhd->kd', dot_grads, query_tile, preferred_element_type=j...  10.9 us
  transfers between devices with their start and end apart: 4, of which 4 were waited for; matrix products, arithmetic and copies ran while one was open for 1% of the time, Pallas kernels for 0%

commit v1 on v0

--- a/solution.py
+++ b/solution.py
@@ -15,7 +15,7 @@
 
 def over_axes(value, axes):
     for axis in axes:
-        value = lax.psum(value, axis)
+        value = jnp.sum(lax.all_gather(value, axis), axis=0)
     return value
 
 

time: 381 us -> 394 us (1.034)
  local copies, waits for them, and re-layouts: 27.4 us -> 39.6 us
  other arithmetic: 57.1 us -> 61.9 us
    psum x4 -> x0, blocking collectives: 40 us -> none  [over_axes(): value = lax.psum(value, axis)]
    unnamed x0 -> x4, blocking collectives: none -> 37.8 us
    unnamed x23 -> x53, local copies, waits for them, and re-layouts: 1.24 us -> 13.4 us
    reduce_sum x0 -> x8, other arithmetic: none -> 4.85 us  [over_axes(): value = jnp.sum(lax.all_gather(value, axis), axis=0)]
  transfers between devices with their start and end apart: 4 -> 4, of which waited for: 4 -> 4; matrix products, arithmetic and copies ran while one was open for 1% -> 2% of each run, Pallas kernels for 0% -> 0%
where the time goes in v1:
time: 394 us; the launch traced here: 392 us
  waiting for transfers between devices  159 us (40%)
  other arithmetic  61.9 us (16%)
  blocking collectives  59.9 us (15%)
  local copies, waits for them, and re-layouts  39.6 us (10%)
  matrix products  37.2 us (9%)
  between operations  18.8 us (5%)
  starting transfers between devices  16.1 us (4%)
    psum x1, waiting for transfers between devices, local(): score_part = lax.psum(partial_value, 'head')  55.2 us
    all_to_all x1, waiting for transfers between devices, local(): lax.all_to_all(spread[tiles_here:].reshape(owner_count, CAP, BLOCK, key_w...  50.3 us
    all_to_all x1, waiting for transfers between devices, local(): lax.all_to_all(reply_blocks, SEQ, split_axis=0, concat_axis=0, tiled=True)  49.8 us
    unnamed x4, blocking collectives  37.8 us
    all_to_all x1, blocking collectives, local(): lax.all_to_all(request, SEQ, split_axis=0, concat_axis=0, tiled=True)  22.1 us
    dot_general x4, matrix products, dot_values(): jnp.einsum('qhd,kd->qhk', query_tile, key_tile.reshape(-1, key_width), pr...  19.5 us
    reduce_sum x2, other arithmetic, backward(): jnp.sum(jnp.maximum(values, 0.0) * grad_tile[:, None, :], axis=2)  14.9 us
    unnamed x53, local copies, waits for them, and re-layouts  13.4 us
  transfers between devices with their start and end apart: 4, of which 4 were waited for; matrix products, arithmetic and copies ran while one was open for 2% of the time, Pallas kernels for 0%

profile of v1, /device:TPU:1, one launch (start us, length us, event | category | flops | bytes accessed | tf_op | source)
XLA Modules:
  0.0 392.4 jit_solution(16988501009234976717)
XLA Ops:
  11.0 22.1 %all_to_all.27 = s32[64,1,1]{2,1,0:T(1,128)S(1)} all-to-all(s32[64,1,1]{2,1,0:T(1,128)S(1)} %copy.39), channel_id=1, replica_groups=mesh['seq_0'=4,'seq_1'=8,'seq_2'=2,'head'=4] {'seq_0','seq_1','seq_2'}, dimensions={0} | all-to-all | bytes 512 | tf_op jit(solution)/shard_map/all_to_all | solution.py:75
  33.1 2.7 fusion.46
  35.8 2.2 gather_fusion.1
  38.0 5.7 %all-to-all-start.1 = ((bf16[64,1,128,128]{3,2,1,0:T(8,128)(2,1)}), bf16[64,1,128,128]{3,2,1,0:T(8,128)(2,1)}, u32[]{:S(2)}, u32[]{:S(2)}) async-start(bf16[64,1,128,128]{3,2,1,0:T(8,128)(2,1)} %bitcast.22), calls=%async_computation.1 | async-start | bytes 4194304 | tf_op jit(solution)/shard_map/all_to_all | solution.py:77
  45.1 49.8 %all-to-all-done.1 = bf16[64,1,128,128]{3,2,1,0:T(8,128)(2,1)} async-done(((bf16[64,1,128,128]{3,2,1,0:T(8,128)(2,1)}), bf16[64,1,128,128]{3,2,1,0:T(8,128)(2,1)}, u32[]{:S(2)}, u32[]{:S(2)}) %all-to-all-start.1) | async-done | bytes 2097184 | tf_op jit(solution)/shard_map/all_to_all | solution.py:77
  94.9 3.1 pad_maximum_fusion
  98.0 2.4 gather_fusion.3
  100.4 8.3 %while.24 = (s32[]{:T(128)}, f32[2,128,2048]{2,1,0:T(8,128)}, bf16[2,128,16,128]{3,1,2,0:T(8,128)(2,1)S(1)}, bf16[2,16,128,128]{3,2,1,0:T(8,128)(2,1)S(1)}, f32[2,128,16]{1,2,0:T(8,128)S(1)}, /*index=5*/s32[]{:T(128)}) while((s32[]{:T(128)}, f32[2,128,2048]{2,1,0:T(8,128)}, bf16[2,128,16,128]{3,1,2,0:T(8,128)(2,1)S(1)}, ...), condition=%wide.region_6.7_spmd, body=%wide.region_4.6_spmd.sunk | while | flops 1086324736 | bytes 22044820 | solution.py:104
  100.5 2.6 multiply_reduce_fusion.4
  103.3 1.3 copy-done.8
  104.6 2.6 multiply_reduce_fusion.4
  107.4 1.3 copy-done.8
  114.0 55.2 %all-reduce.14.cloned.1.call-done = f32[256,2048]{1,0:T(8,128)} async-done(((f32[256,2048]{1,0:T(8,128)}), f32[256,2048]{1,0:T(8,128)}) %all-reduce.14.cloned.1.call-update) | async-done | bytes 2097168 | tf_op jit(solution)/shard_map/psum | solution.py:107
  169.2 2.9 select_reduce_fusion.1
  172.1 3.6 select_reduce_fusion
  179.2 8.4 %all-reduce.10 = (f32[4]{0:T(128)S(1)}, f32[4]{0:T(128)S(1)}) all-reduce(f32[4]{0:T(128)S(1)} %dynamic-update-slice, f32[4]{0:T(128)S(1)} %dynamic-update-slice.4), channel_id=1, replica_groups=mesh['seq_0'=4,'seq_1'=8,'seq_2'=2,'head'=4] {'seq_0'}, use_global_device_ids=true, to_apply=%add | all-reduce | flops 8 | bytes 64
  188.8 1.3 dynamic-update-slice.5
  190.1 1.4 dynamic-update-slice.1
  192.1 13.7 %all-reduce.8 = (f32[8]{0:T(128)S(1)}, f32[8]{0:T(128)S(1)}) all-reduce(f32[8]{0:T(128)S(1)} %dynamic-update-slice.1, f32[8]{0:T(128)S(1)} %dynamic-update-slice.5), channel_id=1, replica_groups=mesh['seq_0'=4,'seq_1'=8,'seq_2'=2,'head'=4] {'seq_1'}, use_global_device_ids=true, to_apply=%add.1 | all-reduce | flops 16 | bytes 128
  207.0 1.3 dynamic-update-slice.6
  208.3 1.5 dynamic-update-slice.2
  210.5 8.7 %all-reduce.11 = (f32[2]{0:T(128)S(1)}, f32[2]{0:T(128)S(1)}) all-reduce(f32[2]{0:T(128)S(1)} %dynamic-update-slice.2, f32[2]{0:T(128)S(1)} %dynamic-update-slice.6), channel_id=1, replica_groups=mesh['seq_0'=4,'seq_1'=8,'seq_2'=2,'head'=4] {'seq_2'}, use_global_device_ids=true, to_apply=%add.2 | all-reduce | flops 4 | bytes 32
  220.4 1.3 dynamic-update-slice.7
  221.7 1.4 dynamic-update-slice.3
  223.7 7.0 %all-reduce.9 = (f32[4]{0:T(128)S(1)}, f32[4]{0:T(128)}) all-reduce(f32[4]{0:T(128)S(1)} %dynamic-update-slice.3, f32[4]{0:T(128)S(1)} %dynamic-update-slice.7), channel_id=1, replica_groups=mesh['seq_0'=4,'seq_1'=8,'seq_2'=2,'head'=4] {'head'}, use_global_device_ids=true, to_apply=%add.3 | all-reduce | flops 8 | bytes 64
  231.3 4.8 %multiply_divide_fusion = f32[256,2048]{1,0:T(8,128)} fusion(f32[256,2048]{1,0:T(8,128)S(1)} %copy-done.1, bf16[256,2048]{1,0:T(8,128)(2,1)} %param.13, f32[]{:T(128)} %reduce_sum.170, f32[256]{0:T(256)S(1)} %get-tuple-element.134, f32[256]{0:T(256)S(1)} %get-tuple-element.132, f32[256]{0:T(256)S(1)} %get-tuple-element.133, pred[32,8,16,128]{3,2,1,0:T(8,128)(4,1)} %bitcast.167), kind=kLoop, calls=%fused_computation.54 | loop fusion | flops 5767168 | bytes 5770244 | tf_op jit(solution)/shard_map/div | solution.py:127
  236.1 54.8 %while.25 = (s32[]{:T(128)}, bf16[2,128,16,128]{3,2,1,0:T(8,128)(2,1)}, f32[2,128,16]{1,0,2:T(2,128)S(1)}, f32[2,16,128,128]{3,2,1,0:T(8,128)}, bf16[2,128,16,12...) while((s32[]{:T(128)}, ...), condition=%wide.region_18.19_spmd, body=%wide.region_16.18_spmd.sunk | while | flops 3313502208 | bytes 53560508 | solution.py:151
  236.1 1.6 dynamic-slice_bitcast_fusion.6
  237.8 7.1 %fusion.74 = (u16[128,2048]{1,0:T(8,128)(2,1)S(1)}, f32[128,16,2048]{2,0,1:T(8,128)}) fusion(bf16[2048,128,1]{1,0,2:T(8,128)(2,1)S(1)} %bitcast.161, bf16[2,128,16,128]{3,1,2,0:T(8,128)(2,1)S(1)} %copy-done.4, s32[]{:T(128)S(6)} %copy.116), kind=kOutput, calls=%fused_computation.21.clone.1 | convolution fusion | flops 1094451200 | bytes 18350084 | tf_op jit(solution)/shard_map/while/body/eval_jaxpr/qhd,kd->qhk/dot_general | solution.py:92
  244.9 3.4 fusion.75
  248.3 7.5 %multiply_reduce_fusion.5 = f32[128,16]{0,1:T(8,128)S(1)} fusion(f32[128,16,2048]{2,0,1:T(8,128)} %get-tuple-element.272, f32[128,2048]{1,0:T(8,128)S(1)} %get-tuple-element.269), kind=kLoop, calls=%fused_computation.19.clone.1 | loop fusion | flops 12580864 | bytes 17833984 | tf_op jit(solution)/shard_map/while/body/eval_jaxpr/reduce_sum | solution.py:134
  255.8 2.2 copy_dynamic-update-slice_fusion.2
  258.0 5.4 %fusion.76 = f32[2,16,128,128]{3,2,1,0:T(8,128)} fusion(f32[2,16,128,128]{3,2,1,0:T(8,128)} %get-tuple-element.306, s32[]{:T(128)S(6)} %copy.116, bf16[2,128,16,128]{3,1,2,0:T(8,128)(2,1)} %get-tuple-element.317, f32[2048,128]{0,1:T(8,128)S(1)} %get-tuple-element.273, f32[16,128]{1,0:T(8,128)S(1)} %get-tuple-element.274, u16[128,2048]{1,0:T(8,128)(2,1)} %copy-done.2), kind=kOutput, calls=%fused_computation.28.clone.1 | convolution fusion | flops 1103101952 | bytes 3154944 | tf_op jit(solution)/shard_map/while/body/eval_jaxpr/qhk,qhd->kd/dot_general | solution.py:146
  263.5 1.6 dynamic-slice_bitcast_fusion.6
  265.1 7.1 %fusion.74 = (u16[128,2048]{1,0:T(8,128)(2,1)S(1)}, f32[128,16,2048]{2,0,1:T(8,128)}) fusion(bf16[2048,128,1]{1,0,2:T(8,128)(2,1)S(1)} %bitcast.161, bf16[2,128,16,128]{3,1,2,0:T(8,128)(2,1)S(1)} %copy-done.4, s32[]{:T(128)S(6)} %copy.116), kind=kOutput, calls=%fused_computation.21.clone.1 | convolution fusion | flops 1094451200 | bytes 18350084 | tf_op jit(solution)/shard_map/while/body/eval_jaxpr/qhd,kd->qhk/dot_general | solution.py:92
  272.2 3.4 fusion.75
  275.6 7.5 %multiply_reduce_fusion.5 = f32[128,16]{0,1:T(8,128)S(1)} fusion(f32[128,16,2048]{2,0,1:T(8,128)} %get-tuple-element.272, f32[128,2048]{1,0:T(8,128)S(1)} %get-tuple-element.269), kind=kLoop, calls=%fused_computation.19.clone.1 | loop fusion | flops 12580864 | bytes 17833984 | tf_op jit(solution)/shard_map/while/body/eval_jaxpr/reduce_sum | solution.py:134
  283.2 2.2 copy_dynamic-update-slice_fusion.2
  285.4 5.5 %fusion.76 = f32[2,16,128,128]{3,2,1,0:T(8,128)} fusion(f32[2,16,128,128]{3,2,1,0:T(8,128)} %get-tuple-element.306, s32[]{:T(128)S(6)} %copy.116, bf16[2,128,16,128]{3,1,2,0:T(8,128)(2,1)} %get-tuple-element.317, f32[2048,128]{0,1:T(8,128)S(1)} %get-tuple-element.273, f32[16,128]{1,0:T(8,128)S(1)} %get-tuple-element.274, u16[128,2048]{1,0:T(8,128)(2,1)} %copy-done.2), kind=kOutput, calls=%fused_computation.28.clone.1 | convolution fusion | flops 1103101952 | bytes 3154944 | tf_op jit(solution)/shard_map/while/body/eval_jaxpr/qhk,qhd->kd/dot_general | solution.py:146
  290.9 2.5 broadcast_in_dim.112
  293.4 6.9 %scatter_fusion = f32[66,128,128]{2,1,0:T(8,128)} fusion(f32[66,128,128]{2,1,0:T(8,128)} %broadcast_in_dim.112, s32[32]{0:T(128)S(1)} %copy-done.13, f32[32,128,128]{2,1,0:T(8,128)S(1)} %bitcast.169), kind=kCustom, calls=%fused_computation.4 | custom fusion | flops 524288 | bytes 6291584 | tf_op jit(solution)/shard_map/scatter-add | solution.py:155
  300.3 3.9 fusion.37
  304.2 6.9 %all-to-all-start.2 = ((bf16[64,1,128,128]{3,2,1,0:T(8,128)(2,1)}), bf16[64,1,128,128]{3,2,1,0:T(8,128)(2,1)S(1)}, u32[]{:S(2)}, u32[]{:S(2)}) async-start(bf16[64,1,128,128]{3,2,1,0:T(8,128)(2,1)} %fusion.37), calls=%async_computation.2 | async-start | bytes 4194304 | tf_op jit(solution)/shard_map/all_to_all | solution.py:158
  312.1 50.3 %all-to-all-done.2 = bf16[64,1,128,128]{3,2,1,0:T(8,128)(2,1)S(1)} async-done(((bf16[64,1,128,128]{3,2,1,0:T(8,128)(2,1)}), bf16[64,1,128,128]{3,2,1,0:T(8,128)(2,1)S(1)}, u32[]{:S(2)}, u32[]{:S(2)}) %all-to-all-start.2) | async-done | bytes 2097184 | tf_op jit(solution)/shard_map/all_to_all | solution.py:158
  362.3 2.5 bitcast_convert_fusion
  364.8 8.8 %scatter_fusion.1 = f32[2,128,128]{2,1,0:T(8,128)S(1)} fusion(f32[2,128,128]{2,1,0:T(8,128)S(1)} %slice.17, s32[64]{0:T(128)S(1)} %copy-done.12, f32[64,128,128]{2,1,0:T(8,128)} %bitcast_convert_fusion), kind=kCustom, calls=%fused_computation.5 | custom fusion | flops 1048576 | bytes 12583168 | tf_op jit(solution)/shard_map/scatter-add | solution.py:165
  374.3 3.4 all-to-all-start.3
  380.3 3.5 all-to-all-done.3
  (125 shorter events, 22.0 us)
Async XLA Ops:
  7.2 28.6 %copy-start = (bf16[256,128]{1,0:T(8,128)(2,1)S(1)}, bf16[256,128]{1,0:T(8,128)(2,1)}, u32[]{:S(2)}) copy-start(bf16[256,128]{1,0:T(8,128)(2,1)} %param.12) | copy-start | bytes 196612
  37.9 6.9 %copy-start.9 = (bf16[256,16,128]{2,1,0:T(8,128)(2,1)S(1)}, bf16[256,16,128]{2,1,0:T(8,128)(2,1)}, u32[]{:S(2)}) copy-start(bf16[256,16,128]{2,1,0:T(8,128)(2,1)} %param.10) | copy-start | bytes 3145732
  38.0 57.0 %all-to-all-start.1 = ((bf16[64,1,128,128]{3,2,1,0:T(8,128)(2,1)}), bf16[64,1,128,128]{3,2,1,0:T(8,128)(2,1)}, u32[]{:S(2)}, u32[]{:S(2)}) async-start(bf16[64,1,128,128]{3,2,1,0:T(8,128)(2,1)} %bitcast.22), calls=%async_computation.1 | async-start | bytes 4194304 | tf_op jit(solution)/shard_map/all_to_all | solution.py:77
  43.7 1.4 copy-start.11
  43.7 125.5 %all-reduce.14.cloned.1.call-start = ((), (), s32[]{:S(2)}) async-start(), calls=%async_computation.4 | async-start | bytes 4194304 | tf_op jit(solution)/shard_map/psum | solution.py:107
  100.5 2.7 copy-start.7
  103.3 1.3 copy-start.8
  104.6 2.7 copy-start.7
  107.4 1.3 copy-start.8
  108.7 5.3 %copy-start.3 = (bf16[2,128,16,128]{3,1,2,0:T(8,128)(2,1)}, bf16[2,128,16,128]{3,1,2,0:T(8,128)(2,1)S(1)}, u32[]{:S(2)}) copy-start(bf16[2,128,16,128]{3,1,2,0:T(8,128)(2,1)S(1)} %get-tuple-element.326) | copy-start | bytes 3145732
  108.7 0.7 copy-start.14
  108.7 0.7 copy-start.18
  108.7 1.3 copy-start.10
  169.2 2.9 copy-start.1
  169.2 2.9 copy-start.5
  172.1 6.5 %copy-start.17 = (u32[256]{0:T(256)S(1)}, u32[256]{0:T(256)}, u32[]{:S(2)}) copy-start(u32[256]{0:T(256)} %constant.152) | copy-start | bytes 3076
  172.1 19.4 %copy-start.16 = (u32[256]{0:T(256)S(1)}, u32[256]{0:T(256)}, u32[]{:S(2)}) copy-start(u32[256]{0:T(256)} %constant.157) | copy-start | bytes 3076
  172.1 37.7 %copy-start.15 = (u32[256]{0:T(256)S(1)}, u32[256]{0:T(256)}, u32[]{:S(2)}) copy-start(u32[256]{0:T(256)} %constant.162) | copy-start | bytes 3076
  236.1 1.6 copy-start.4
  244.9 3.4 copy-start.2
  263.5 1.6 copy-start.4
  272.2 3.4 copy-start.2
  290.9 2.5 copy-start.6
  290.9 2.5 copy-start.13
  304.2 58.1 %all-to-all-start.2 = ((bf16[64,1,128,128]{3,2,1,0:T(8,128)(2,1)}), bf16[64,1,128,128]{3,2,1,0:T(8,128)(2,1)S(1)}, u32[]{:S(2)}, u32[]{:S(2)}) async-start(bf16[64,1,128,128]{3,2,1,0:T(8,128)(2,1)} %fusion.37), calls=%async_computation.2 | async-start | bytes 4194304 | tf_op jit(solution)/shard_map/all_to_all | solution.py:158
  312.0 52.7 %copy-start.12 = (s32[64]{0:T(128)S(1)}, s32[64]{0:T(128)}, u32[]{:S(2)}) copy-start(s32[64]{0:T(128)} %get-tuple-element.135) | copy-start | bytes 772
  364.8 12.9 %copy-start.19 = (f32[4]{0:T(128)S(1)}, f32[4]{0:T(128)}, u32[]{:S(2)}) copy-start(f32[4]{0:T(128)} %get-tuple-element.166) | copy-start | bytes 52
  374.3 9.4 %all-to-all-start.3 = ((bf16[4,2,128,128]{3,2,1,0:T(8,128)(2,1)}), bf16[4,2,128,128]{3,2,1,0:T(8,128)(2,1)S(1)}, u32[]{:S(2)}, u32[]{:S(2)}) async-start(bf16[4,2,128,128]{3,2,1,0:T(8,128)(2,1)} %broadcast_in_dim.113), calls=%async_computation.3 | async-start | bytes 524288 | tf_op jit(solution)/shard_map/all_to_all | solution.py:24
Sparse Core Ops, SparseCore 0:
  108.9 60.2 all-reduce.13
